TPU v7x, 32 devices: a whole 2x2x4 slice. The times are simulated.
32 devices in a mesh: grp: 2 (over y), ia: 4 (over z), ja: 4 (over x, core).
Axes of the slice: x: 2, y: 2, z: 4, core: 2. Of those that a mesh axis runs over, the one named last changes fastest.
Arguments:
- doubles: bfloat16 [8, 16, 384, 384], P(('grp', 'ia'), 'ja'), parts along dimension 0, may hold values from -6 to 6
- aux_factors: bfloat16 [4, 384, 384], P('ia'), may hold values from -0.15625 to 0.15625
- cycle_factors: bfloat16 [16, 384, 128], replicated, may hold values from -0.21875 to 0.21875
Outputs:
- sigma: bfloat16 [8, 16, 384, 384], P(('grp', 'ia'), 'ja'), parts along dimension 0
There are 2 independent parts, one for each index of `grp`. A program takes and returns all parts, laid end to end along the dimension named above; an argument that names none is the same for every part. Nothing has to cross between parts.
All inputs are finite; a program needn't handle non-finite values.
Results may differ from a plain program's by a relative error of at most 0.008.
Values may be sent and summed in bfloat16 or wider, within the bound.
A program may use at most 128 MiB of HBM per device.

v0:
```python
import jax
import jax.numpy as jnp
from jax import lax
from jax.sharding import PartitionSpec as P


def ladder_terms(pair_blocks, factor):
    halfway = jnp.einsum(
        "pcd,bd->pcb", pair_blocks, factor, preferred_element_type=jnp.float32
    ).astype(jnp.bfloat16)
    return jnp.einsum("ac,pcb->pab", factor, halfway, preferred_element_type=jnp.float32)


def add_factors(running, pair_blocks, factors):

    def one_step(position, acc):
        factor = lax.dynamic_index_in_dim(factors, position, 0, keepdims=False)
        return acc + ladder_terms(pair_blocks, factor)

    return lax.fori_loop(0, factors.shape[0], one_step, running)


def shards(doubles, aux_factors, cycle_factors):
    rows_i, cols_j, width, _ = doubles.shape
    pair_blocks = doubles.reshape(rows_i * cols_j, width, width)
    zeros_acc = jnp.zeros((rows_i * cols_j, width, width), jnp.float32)
    ladder = add_factors(
        zeros_acc, pair_blocks, lax.all_gather(aux_factors, "ia", axis=0, tiled=True)
    )
    ladder = ladder.reshape(rows_i, cols_j, width, width)
    offset = lax.axis_index("ja") * cols_j
    local_factors = lax.dynamic_slice_in_dim(cycle_factors, offset, cols_j, 0)
    partial_latent = jnp.einsum(
        "ijab,jbq->iaq", doubles, local_factors, preferred_element_type=jnp.float32
    )
    latent = lax.psum(partial_latent, "ja").astype(jnp.bfloat16)
    cycle_term = jnp.einsum(
        "iaq,jbq->ijab", latent, local_factors, preferred_element_type=jnp.float32
    ).astype(jnp.bfloat16)
    return (ladder + cycle_term.astype(jnp.float32)).astype(jnp.bfloat16)


def solution(mesh):
    in_specs = (P(("grp", "ia"), "ja", None, None), P("ia", None, None), P())
    out_specs = P(("grp", "ia"), "ja", None, None)
    return jax.shard_map(shards, mesh=mesh, in_specs=in_specs, out_specs=out_specs, check_vma=False)
```

profile of v0, /device:TPU:0, one launch (start us, length us, event | category | flops | bytes accessed | tf_op | source)
XLA Modules:
  0.0 70.7 jit_solution(2368934704128992936)
XLA Ops:
  6.5 0.0 copy-start
  6.5 0.0 copy-start.1
  6.5 0.0 all-gather.2.cloned.1.call-start
  6.5 0.7 %all-gather.2.cloned.1.call-update = ((bf16[1,384,384]{2,1,0:T(8,128)(2,1)}), bf16[4,384,384]{2,1,0:T(8,128)(2,1)}) async-update(((), (), s32[]{:S(2)}) %all-gather.2.cloned.1.call-start, bf16[1,384,384]{2,1,0:T(8,128)(2,1)} %param.6) | async-update | bytes 1769496
  7.3 0.7 copy-done
  7.9 1.8 %convolution_bitcast_fusion = f32[1,384,128]{1,2,0:T(8,128)S(1)} fusion(bf16[16,384,128]{2,1,0:T(8,128)(2,1)S(1)} %copy-done, s32[]{:T(128)S(6)} %select_n.9, bf16[1,4,384,384]{3,2,1,0:T(8,128)(2,1)} %param.5), kind=kOutput, calls=%fused_computation.11 | convolution fusion | flops 150994944 | bytes 1769476 | tf_op jit(solution)/shard_map/ijab,jbq->iaq/dot_general | solution.py:33
  9.7 15.3 %all-reduce.1 = bf16[1,384,128]{1,2,0:T(8,128)(2,1)S(1)} all-reduce(f32[1,384,128]{1,2,0:T(8,128)S(1)} %convolution_bitcast_fusion), channel_id=1, replica_groups=mesh['grp'=2,'ia'=4,'ja'=4] {'ja'}, use_global_device_ids=true, to_apply=%region_2.3 | all-reduce | flops 49152 | bytes 294912 | tf_op jit(solution)/shard_map/psum | solution.py:36
  25.0 16.9 %all-gather.2.cloned.1.call-done = bf16[4,384,384]{2,1,0:T(8,128)(2,1)} async-done(((bf16[1,384,384]{2,1,0:T(8,128)(2,1)}), bf16[4,384,384]{2,1,0:T(8,128)(2,1)}) %all-gather.2.cloned.1.call-update) | async-done | bytes 1179664 | tf_op jit(solution)/shard_map/all_gather | solution.py:28
  41.9 0.0 copy-done.1
  41.9 18.4 %while.14 = (s32[]{:T(128)}, f32[4,384,384]{1,2,0:T(8,128)}, bf16[4,384,384]{2,1,0:T(8,128)(2,1)}, bf16[4,384,384]{2,1,0:T(8,128)(2,1)S(1)}, s32[]{:T(128)}, /*index=5*/s32[]{:T(128)}) while((s32[]{:T(128)}, f32[4,384,384]{1,2,0:T(8,128)}, bf16[4,384,384]{2,1,0:T(8,128)(2,1)}, bf16[4,384,384]{2,1,0:T(8,128)(2,1)S(1)}, s32[]{:T(128)}, ...), condition=%wide.region_1.2_spmd.clone, body=%wide.region_0.1_spmd.clone.sunk | while | flops 907739136 | bytes 6489686 | solution.py:20
  41.9 4.0 %bitcast_add_fusion.2 = f32[4,384,384]{1,2,0:T(8,128)} fusion(f32[4,384,384]{1,2,0:T(8,128)} %get-tuple-element.140, bf16[4,384,384]{2,1,0:T(8,128)(2,1)S(1)} %get-tuple-element.148, pred[]{:T(512)S(6)} %compare.3, bf16[4,384,384]{2,1,0:T(8,128)(2,1)} %get-tuple-element.147, s32[]{:T(128)S(6)} %copy.18), kind=kOutput, calls=%fused_computation.clone.1 | convolution fusion | flops 907739136 | bytes 6489600 | tf_op jit(solution)/shard_map/while/body/eval_jaxpr/ac,pcb->pab/dot_general | solution.py:11
  45.9 4.8 %bitcast_add_fusion.2 = f32[4,384,384]{1,2,0:T(8,128)} fusion(f32[4,384,384]{1,2,0:T(8,128)} %get-tuple-element.140, bf16[4,384,384]{2,1,0:T(8,128)(2,1)S(1)} %get-tuple-element.148, pred[]{:T(512)S(6)} %compare.3, bf16[4,384,384]{2,1,0:T(8,128)(2,1)} %get-tuple-element.147, s32[]{:T(128)S(6)} %copy.18), kind=kOutput, calls=%fused_computation.clone.1 | convolution fusion | flops 907739136 | bytes 6489600 | tf_op jit(solution)/shard_map/while/body/eval_jaxpr/ac,pcb->pab/dot_general | solution.py:11
  50.7 4.8 %bitcast_add_fusion.2 = f32[4,384,384]{1,2,0:T(8,128)} fusion(f32[4,384,384]{1,2,0:T(8,128)} %get-tuple-element.140, bf16[4,384,384]{2,1,0:T(8,128)(2,1)S(1)} %get-tuple-element.148, pred[]{:T(512)S(6)} %compare.3, bf16[4,384,384]{2,1,0:T(8,128)(2,1)} %get-tuple-element.147, s32[]{:T(128)S(6)} %copy.18), kind=kOutput, calls=%fused_computation.clone.1 | convolution fusion | flops 907739136 | bytes 6489600 | tf_op jit(solution)/shard_map/while/body/eval_jaxpr/ac,pcb->pab/dot_general | solution.py:11
  55.5 4.8 %bitcast_add_fusion.2 = f32[4,384,384]{1,2,0:T(8,128)} fusion(f32[4,384,384]{1,2,0:T(8,128)} %get-tuple-element.140, bf16[4,384,384]{2,1,0:T(8,128)(2,1)S(1)} %get-tuple-element.148, pred[]{:T(512)S(6)} %compare.3, bf16[4,384,384]{2,1,0:T(8,128)(2,1)} %get-tuple-element.147, s32[]{:T(128)S(6)} %copy.18), kind=kOutput, calls=%fused_computation.clone.1 | convolution fusion | flops 907739136 | bytes 6489600 | tf_op jit(solution)/shard_map/while/body/eval_jaxpr/ac,pcb->pab/dot_general | solution.py:11
  60.3 2.1 %fusion.8 = bf16[1,4,384,384]{2,3,1,0:T(8,128)(2,1)S(1)} fusion(f32[4,384,384]{1,2,0:T(8,128)} %get-tuple-element.84, bf16[16,384,128]{2,1,0:T(8,128)(2,1)S(1)} %copy-done, s32[]{:T(128)S(6)} %select_n.9, bf16[1,384,128]{1,2,0:T(8,128)(2,1)S(1)} %all-reduce.1), kind=kOutput, calls=%fused_computation.8 | convolution fusion | flops 153354240 | bytes 4030468 | tf_op jit(solution)/shard_map/iaq,jbq->ijab/dot_general | solution.py:37
  62.4 1.5 %copy.11 = bf16[1,4,384,384]{3,2,1,0:T(8,128)(2,1)} copy(bf16[1,4,384,384]{2,3,1,0:T(8,128)(2,1)S(1)} %fusion.8) | data formatting | bytes 2359296 | tf_op jit(solution)/shard_map/convert_element_type | solution.py:40
  (1 shorter events, 0.0 us)
Async XLA Ops:
  6.5 1.4 %copy-start = (bf16[16,384,128]{2,1,0:T(8,128)(2,1)S(1)}, bf16[16,384,128]{2,1,0:T(8,128)(2,1)}, u32[]{:S(2)}) copy-start(bf16[16,384,128]{2,1,0:T(8,128)(2,1)} %param.7) | copy-start | bytes 4718596
  6.5 35.4 %copy-start.1 = (bf16[1,4,384,384]{3,2,1,0:T(8,128)(2,1)S(1)}, bf16[1,4,384,384]{3,2,1,0:T(8,128)(2,1)}, u32[]{:S(2)}) copy-start(bf16[1,4,384,384]{3,2,1,0:T(8,128)(2,1)} %param.5) | copy-start | bytes 3538948
  6.5 35.4 %all-gather.2.cloned.1.call-start = ((), (), s32[]{:S(2)}) async-start(), calls=%async_computation | async-start | bytes 1474560 | tf_op jit(solution)/shard_map/all_gather | solution.py:28
Sparse Core Ops, SparseCore 0:
  8.9 32.9 all-gather.1
where the time goes:
time: 71 us; the launch traced here: 70.7 us
  matrix products  22.2 us (31%)
  waiting for transfers between devices  17.6 us (25%)
  blocking collectives  15.3 us (22%)
  between operations  13.4 us (19%)
  local copies, waits for them, and re-layouts  2.13 us (3%)
    dot_general x4, matrix products, ladder_terms(): jnp.einsum('ac,pcb->pab', factor, halfway, preferred_element_type=jnp.flo...  18.4 us
    all_gather x1, waiting for transfers between devices, shards(): lax.all_gather(aux_factors, 'ia', axis=0, tiled=True)  16.9 us
    psum x1, blocking collectives, shards(): latent = lax.psum(partial_latent, 'ja').astype(jnp.bfloat16)  15.3 us
    dot_general x1, matrix products, shards(): jnp.einsum('iaq,jbq->ijab', latent, local_factors, preferred_element_type...  2.11 us
    dot_general x1, matrix products, shards(): jnp.einsum('ijab,jbq->iaq', doubles, local_factors, preferred_element_typ...  1.77 us
    convert_element_type x1, local copies, waits for them, and re-layouts, shards(): return (ladder + cycle_term.astype(jnp.float32)).astype(jnp.bfloat16)  1.45 us
  transfers between devices with their start and end apart: 1, of which 1 were waited for; matrix products, arithmetic and copies ran while one was open for 2% of the time, Pallas kernels for 0%

commit v1 on v0

v1 whole, which is shorter than its diff:
```python
import functools

import jax
import jax.numpy as jnp
from jax import lax
from jax.experimental import pallas as pl
from jax.experimental.pallas import tpu as pltpu
from jax.sharding import PartitionSpec as P

MESH = pl.DeviceIdType.MESH
F32 = jnp.float32
BF16 = jnp.bfloat16
NT = (((1,), (1,)), ((), ()))
CORES = 2


def sigma_kernel(n, nj, d_hbm, aux_hbm, u_hbm, out_hbm, d, u, aux, half, acc, out,
                 plat, lat_in, lat, load_sem, out_sem, z_send, z_recv, x_send, x_recv,
                 s_send, s_recv, p_send, p_recv, l_send, l_recv):
    nx = nj // CORES
    pairs_j, width = d.shape[0], d.shape[1]
    grp_j = half.shape[2] // width
    n_jp = pairs_j // grp_j
    rows = width // nj
    iz = lax.axis_index("ia")
    ij = lax.axis_index("ja")
    sibling = ij ^ 1

    def chunk(owner):
        return pl.ds(pl.multiple_of(owner * rows, rows), rows)

    def slot(k):
        return pl.ds(k * width, width)

    load_aux = pltpu.make_async_copy(aux_hbm.at[0], aux.at[:, slot(0)], load_sem.at[0])
    load_d = pltpu.make_async_copy(d_hbm.at[0], d, load_sem.at[1])
    load_u = pltpu.make_async_copy(
        u_hbm.at[pl.ds(ij * pairs_j, pairs_j)], u, load_sem.at[2])
    load_aux.start()
    load_d.start()
    load_u.start()

    barrier = pltpu.get_barrier_semaphore()
    for k in range(1, n):
        pl.semaphore_signal(barrier, inc=1, device_id={"ia": iz ^ k}, device_id_type=MESH)
    for m in range(1, nj):
        pl.semaphore_signal(barrier, inc=1, device_id={"ja": ij ^ m}, device_id_type=MESH)
    pl.semaphore_wait(barrier, n - 1 + nj - 1)

    def remote(src, dst, send, recv, where):
        return pltpu.make_async_remote_copy(
            src_ref=src, dst_ref=dst, send_sem=send, recv_sem=recv,
            device_id=where, device_id_type=MESH)

    def z_copy(k):
        return remote(aux.at[chunk(ij), slot(0)], aux.at[chunk(ij), slot(k)],
                      z_send.at[k], z_recv.at[k], {"ia": iz ^ k})

    def x_copy(k, m, owner):
        part = aux.at[chunk(owner), slot(k)]
        return remote(part, part, x_send.at[k, m], x_recv.at[k, m],
                      {"ja": ij ^ (CORES * m)})

    def s_copy(k, m, owner):
        part = aux.at[chunk(owner), slot(k)]
        return remote(part, part, s_send.at[k, m], s_recv.at[k, m], {"ja": sibling})

    def p_copy(m):
        return remote(plat.at[chunk(ij ^ m)], lat_in.at[m], p_send.at[m], p_recv.at[m],
                      {"ja": ij ^ m})

    def l_copy(m, owner):
        return remote(lat.at[chunk(owner)], lat.at[chunk(owner)], l_send.at[m],
                      l_recv.at[m], {"ja": ij ^ m})

    load_aux.wait()
    for k in range(1, n):
        z_copy(k).start()

    load_d.wait()
    load_u.wait()

    total = jnp.zeros(plat.shape, F32)
    for j in range(pairs_j):
        total += jnp.dot(d[j], u[j], preferred_element_type=F32)
    plat[...] = total.astype(BF16)

    def halfway(k, place):
        factor = aux[:, k * width:(k + 1) * width]

        @pl.loop(0, n_jp)
        def _(jp):
            for t in range(grp_j):
                block = lax.dot_general(d[jp * grp_j + t], factor, NT,
                                        preferred_element_type=F32)
                half[jp, place * width:(place + 1) * width,
                     t * width:(t + 1) * width] = block.astype(BF16)

    halfway(0, 0)
    for m in range(1, nj):
        p_copy(m).start()

    def pass_on(k):
        z_copy(k).wait_recv()
        for m in range(1, nx):
            x_copy(k, m, ij).start()
        s_copy(k, 0, ij).start()

    def gather_latent():
        mine = plat[chunk(ij), :].astype(F32)
        for m in range(1, nj):
            p_copy(m).wait_recv()
            mine += lat_in[m].astype(F32)
        lat[chunk(ij), :] = mine.astype(BF16)

    def send_latent():
        for m in range(1, nj):
            l_copy(m, ij).start()

    def ladder(first, count, last):
        @pl.loop(0, n_jp)
        def _(jp):
            res = jnp.dot(aux[:, first * width:(first + count) * width],
                          half[jp, :count * width, :], preferred_element_type=F32)
            if first > 0:
                res += acc[jp]
            if not last:
                acc[jp] = res
            else:
                for t in range(grp_j):
                    j = jp * grp_j + t
                    cyc = lax.dot_general(lat[...], u[j], NT, preferred_element_type=F32)
                    out[j] = (res[:, t * width:(t + 1) * width] + cyc).astype(BF16)
                    pltpu.make_async_copy(out.at[j], out_hbm.at[0, j], out_sem.at[j]).start()

    def latent_all():
        for m in range(1, nj):
            l_copy(m, ij ^ m).wait_recv()

    if n > 1:
        pass_on(1)
    gather_latent()
    if n == 1:
        send_latent()
        latent_all()
        ladder(0, 1, True)
    for k in range(1, n):
        if k + 1 < n:
            pass_on(k + 1)
        if k == 1:
            send_latent()
        for m in range(1, nx):
            x_copy(k, m, ij ^ (CORES * m)).wait_recv()
            s_copy(k, m, ij ^ (CORES * m)).start()
        for m in range(nx):
            s_copy(k, m, sibling ^ (CORES * m)).wait_recv()
        halfway(k, k % 2)
        if k == n - 1:
            latent_all()
        if k % 2 == 1:
            ladder(k - 1, 2, k == n - 1)
        elif k == n - 1:
            ladder(k, 1, True)

    for j in range(pairs_j):
        pltpu.make_async_copy(out.at[j], out_hbm.at[0, j], out_sem.at[j]).wait()
    for k in range(1, n):
        z_copy(k).wait_send()
        for m in range(1, nx):
            x_copy(k, m, ij).wait_send()
        for m in range(nx):
            s_copy(k, m, ij ^ (CORES * m)).wait_send()
    for m in range(1, nj):
        p_copy(m).wait_send()
        l_copy(m, ij).wait_send()


def shards(n, nj, doubles, aux_factors, cycle_factors):
    _, pairs_j, width, _ = doubles.shape
    rank = cycle_factors.shape[2]
    grp_j = 2 if pairs_j % 2 == 0 else 1
    nx = nj // CORES
    dma = pltpu.SemaphoreType.DMA
    hbm = pl.BlockSpec(memory_space=pltpu.HBM)
    flops = 4 * n * pairs_j * width**3 + 4 * pairs_j * width * width * rank
    return pl.pallas_call(
        functools.partial(sigma_kernel, n, nj),
        out_shape=jax.ShapeDtypeStruct(doubles.shape, BF16),
        in_specs=[hbm] * 3,
        out_specs=hbm,
        scratch_shapes=[
            pltpu.VMEM((pairs_j, width, width), BF16),
            pltpu.VMEM((pairs_j, width, rank), BF16),
            pltpu.VMEM((width, n * width), BF16),
            pltpu.VMEM((pairs_j // grp_j, 2 * width, grp_j * width), BF16),
            pltpu.VMEM((pairs_j // grp_j, width, grp_j * width), F32),
            pltpu.VMEM((pairs_j, width, width), BF16),
            pltpu.VMEM((width, rank), BF16),
            pltpu.VMEM((nj, width // nj, rank), BF16),
            pltpu.VMEM((width, rank), BF16),
            dma((3,)),
            dma((pairs_j,)),
            dma((n,)), dma((n,)),
            dma((n, nx)), dma((n, nx)),
            dma((n, nx)), dma((n, nx)),
            dma((nj,)), dma((nj,)),
            dma((nj,)), dma((nj,)),
        ],
        compiler_params=pltpu.CompilerParams(
            collective_id=0, has_side_effects=True, vmem_limit_bytes=56 * 2**20),
        cost_estimate=pl.CostEstimate(
            flops=flops, bytes_accessed=4 * doubles.size, transcendentals=0),
    )(doubles, aux_factors, cycle_factors)


def solution(mesh):
    in_specs = (P(("grp", "ia"), "ja", None, None), P("ia", None, None), P())
    out_specs = P(("grp", "ia"), "ja", None, None)
    body = functools.partial(shards, mesh.shape["ia"], mesh.shape["ja"])
    return jax.shard_map(body, mesh=mesh, in_specs=in_specs, out_specs=out_specs, check_vma=False)
```

time: 71 us -> 26.9 us (0.38)
  Pallas kernels: 0 us -> 24.4 us
  matrix products: 22.2 us -> 0 us
  waiting for transfers between devices: 17.6 us -> 0 us
  blocking collectives: 15.3 us -> 0 us
  between operations: 13.4 us -> 0.01 us
    pallas_call x0 -> x1, Pallas kernels: none -> 24.4 us  [shards(): pl.pallas_call(functools.partial(sigma_kernel, n, nj), out_shape=jax.Shap...]
    dot_general x6 -> x0, matrix products: 22.2 us -> none  [the longest x4 18.4 us: ladder_terms(): jnp.einsum('ac,pcb->pab', factor, halfway, preferred_element_type=jnp.flo...]
    all_gather x1 -> x0, waiting for transfers between devices: 16.9 us -> none  [shards(): lax.all_gather(aux_factors, 'ia', axis=0, tiled=True)]
    psum x1 -> x0, blocking collectives: 15.3 us -> none  [shards(): latent = lax.psum(partial_latent, 'ja').astype(jnp.bfloat16)]
    unnamed x4 -> x1, local copies, waits for them, and re-layouts: 0.67 us -> 2.4 us
    convert_element_type x1 -> x0, local copies, waits for them, and re-layouts: 1.45 us -> none  [shards(): return (ladder + cycle_term.astype(jnp.float32)).astype(jnp.bfloat16)]
    unnamed x1 -> x0, waiting for transfers between devices: 0.71 us -> none
  transfers between devices with their start and end apart: 1 -> 0, of which waited for: 1 -> 0; matrix products, arithmetic and copies ran while one was open for 2% -> 0% of each run, Pallas kernels for 0% -> 0%
where the time goes in v1:
time: 26.9 us; the launch traced here: 26.8 us
  Pallas kernels  24.4 us (91%)
  local copies, waits for them, and re-layouts  2.4 us (9%)
    pallas_call x1, Pallas kernels, shards(): pl.pallas_call(functools.partial(sigma_kernel, n, nj), out_shape=jax.Shap...  24.4 us
    unnamed x1, local copies, waits for them, and re-layouts  2.4 us

profile of v1, /device:TPU:0, one launch (start us, length us, event | category | flops | bytes accessed | tf_op | source)
XLA Modules:
  0.0 26.8 jit_solution(11492525416575518909)
XLA Ops:
  0.0 24.4 %shard_map.37 = bf16[1,4,384,384]{3,2,1,0:T(8,128)(2,1)} custom-call(bf16[1,4,384,384]{3,2,1,0:T(8,128)(2,1)} %d_hbm.1, bf16[1,384,384]{2,1,0:T(8,128)(2,1)} %aux_hbm.1, bf16[16,384,128]{2,1,0:T(8,128)(2,1)} %u_hbm.1), custom_call_target="tpu_custom_call" | custom-call | flops 3925868544 | bytes 2359296 | tf_op jit(solution)/shard_map/pallas_call | solution.py:186
  24.4 2.4 %copy.5 = bf16[1,4,384,384]{3,2,1,0:T(8,128)(2,1)} copy(bf16[1,4,384,384]{3,2,1,0:T(8,128)(2,1)} %shard_map.37) | data formatting | bytes 2359296

commit v2 on v1

v2 whole, which is shorter than its diff:
```python
import functools

import jax
import jax.numpy as jnp
from jax import lax
from jax.experimental import pallas as pl
from jax.experimental.pallas import tpu as pltpu
from jax.sharding import PartitionSpec as P

MESH = pl.DeviceIdType.MESH
F32 = jnp.float32
BF16 = jnp.bfloat16
NT = (((1,), (1,)), ((), ()))
CORES = 2


def sigma_kernel(n, nj, ny, d_hbm, aux_hbm, u_hbm, out, d, u, aux, half, acc,
                 plat, lat_in, lat, load_sem, z_send, z_recv, x_send, x_recv,
                 s_send, s_recv, p_send, p_recv, l_send, l_recv):
    nx = nj // CORES
    pairs_j, width = d.shape[0], d.shape[1]
    grp_j = half.shape[2] // width
    n_jp = pairs_j // grp_j
    rows = width // (ny * nj)
    lat_rows = width // nj
    iz = lax.axis_index("ia")
    iy = lax.axis_index("grp") if ny > 1 else 0
    ij = lax.axis_index("ja")
    sibling = ij ^ 1

    def chunk(owner):
        return pl.ds(pl.multiple_of(owner * rows, rows), rows)

    def lat_chunk(owner):
        return pl.ds(pl.multiple_of(owner * lat_rows, lat_rows), lat_rows)

    def piece(m, base):
        return chunk((iy ^ (m // nx)) * nj + (base ^ (CORES * (m % nx))))

    def slot(k):
        return pl.ds(k * width, width)

    load_aux = pltpu.make_async_copy(aux_hbm.at[0], aux.at[:, slot(0)], load_sem.at[0])
    load_d = pltpu.make_async_copy(d_hbm.at[0], d, load_sem.at[1])
    load_u = pltpu.make_async_copy(
        u_hbm.at[pl.ds(ij * pairs_j, pairs_j)], u, load_sem.at[2])
    load_aux.start()
    load_d.start()
    load_u.start()

    def plane(m):
        where = {"ja": ij ^ (CORES * (m % nx))}
        if m >= nx:
            where["grp"] = iy ^ (m // nx)
        return where

    barrier = pltpu.get_barrier_semaphore()
    for k in range(1, n):
        pl.semaphore_signal(barrier, inc=1, device_id={"ia": iz ^ k}, device_id_type=MESH)
    for m in range(1, nj):
        pl.semaphore_signal(barrier, inc=1, device_id={"ja": ij ^ m}, device_id_type=MESH)
    for m in range(nx, ny * nx):
        pl.semaphore_signal(barrier, inc=1, device_id=plane(m), device_id_type=MESH)
    pl.semaphore_wait(barrier, n - 1 + nj - 1 + (ny - 1) * nx)

    def remote(src, dst, send, recv, where):
        return pltpu.make_async_remote_copy(
            src_ref=src, dst_ref=dst, send_sem=send, recv_sem=recv,
            device_id=where, device_id_type=MESH)

    def z_copy(k):
        return remote(aux.at[piece(0, ij), slot(0)], aux.at[piece(0, ij), slot(k)],
                      z_send.at[k], z_recv.at[k], {"ia": iz ^ k})

    def x_copy(k, m, from_m=0):
        part = aux.at[piece(from_m, ij), slot(k)]
        return remote(part, part, x_send.at[k, m], x_recv.at[k, m], plane(m))

    def s_copy(k, m, base):
        part = aux.at[piece(m, base), slot(k)]
        return remote(part, part, s_send.at[k, m], s_recv.at[k, m], {"ja": sibling})

    def p_copy(m):
        return remote(plat.at[lat_chunk(ij ^ m)], lat_in.at[m], p_send.at[m], p_recv.at[m],
                      {"ja": ij ^ m})

    def l_copy(m, owner):
        return remote(lat.at[lat_chunk(owner)], lat.at[lat_chunk(owner)], l_send.at[m],
                      l_recv.at[m], {"ja": ij ^ m})

    load_aux.wait()
    for k in range(1, n):
        z_copy(k).start()

    load_d.wait()
    load_u.wait()

    total = jnp.zeros(plat.shape, F32)
    for j in range(pairs_j):
        total += jnp.dot(d[j], u[j], preferred_element_type=F32)
    plat[...] = total.astype(BF16)

    def halfway(k, place):
        factor = aux[:, k * width:(k + 1) * width]

        @pl.loop(0, n_jp)
        def _(jp):
            for t in range(grp_j):
                block = lax.dot_general(d[jp * grp_j + t], factor, NT,
                                        preferred_element_type=F32)
                half[jp, place * width:(place + 1) * width,
                     t * width:(t + 1) * width] = block.astype(BF16)

    halfway(0, 0)
    for m in range(1, nj):
        p_copy(m).start()

    passed, relayed = set(), set()

    def pass_on(k):
        if k >= n or k in passed:
            return
        passed.add(k)
        z_copy(k).wait_recv()
        for m in range(1, ny * nx):
            x_copy(k, m).start()
        s_copy(k, 0, ij).start()

    def relay(k):
        if k >= n or k in relayed:
            return
        relayed.add(k)
        for m in range(1, ny * nx):
            x_copy(k, m, m).wait_recv()
            s_copy(k, m, ij).start()

    def gather_latent():
        mine = plat[lat_chunk(ij), :].astype(F32)
        for m in range(1, nj):
            p_copy(m).wait_recv()
            mine += lat_in[m].astype(F32)
        lat[lat_chunk(ij), :] = mine.astype(BF16)

    def send_latent():
        for m in range(1, nj):
            l_copy(m, ij).start()

    def ladder(first, count, last):
        @pl.loop(0, n_jp)
        def _(jp):
            res = jnp.dot(aux[:, first * width:(first + count) * width],
                          half[jp, :count * width, :], preferred_element_type=F32)
            if first > 0:
                res += acc[jp]
            if not last:
                acc[jp] = res
            else:
                for t in range(grp_j):
                    j = jp * grp_j + t
                    cyc = lax.dot_general(lat[...], u[j], NT, preferred_element_type=F32)
                    out[0, j] = (res[:, t * width:(t + 1) * width] + cyc).astype(BF16)

    def latent_all():
        for m in range(1, nj):
            l_copy(m, ij ^ m).wait_recv()

    pass_on(1)
    pass_on(2)
    gather_latent()
    relay(1)
    pass_on(3)
    send_latent()
    if n == 1:
        latent_all()
        ladder(0, 1, True)
    for k in range(1, n):
        for m in range(ny * nx):
            s_copy(k, m, sibling).wait_recv()
        halfway(k, k % 2)
        relay(k + 1)
        pass_on(k + 3)
        if k == n - 1:
            latent_all()
        if k % 2 == 1:
            relay(k + 2)
            ladder(k - 1, 2, k == n - 1)
        elif k == n - 1:
            ladder(k, 1, True)

    for k in range(1, n):
        z_copy(k).wait_send()
        for m in range(1, ny * nx):
            x_copy(k, m).wait_send()
        for m in range(ny * nx):
            s_copy(k, m, ij).wait_send()
    for m in range(1, nj):
        p_copy(m).wait_send()
        l_copy(m, ij).wait_send()


def shards(n, nj, grps, doubles, aux_factors, cycle_factors):
    _, pairs_j, width, _ = doubles.shape
    rank = cycle_factors.shape[2]
    grp_j = 2 if pairs_j % 2 == 0 else 1
    ny = grps if width % (grps * nj * 16) == 0 else 1
    nx = nj // CORES * ny
    dma = pltpu.SemaphoreType.DMA
    hbm = pl.BlockSpec(memory_space=pltpu.HBM)
    flops = 4 * n * pairs_j * width**3 + 4 * pairs_j * width * width * rank
    return pl.pallas_call(
        functools.partial(sigma_kernel, n, nj, ny),
        out_shape=pltpu.VMEM(doubles.shape, BF16),
        in_specs=[hbm] * 3,
        out_specs=pl.BlockSpec(memory_space=pltpu.VMEM),
        scratch_shapes=[
            pltpu.VMEM((pairs_j, width, width), BF16),
            pltpu.VMEM((pairs_j, width, rank), BF16),
            pltpu.VMEM((width, n * width), BF16),
            pltpu.VMEM((pairs_j // grp_j, 2 * width, grp_j * width), BF16),
            pltpu.VMEM((pairs_j // grp_j, width, grp_j * width), F32),
            pltpu.VMEM((width, rank), BF16),
            pltpu.VMEM((nj, width // nj, rank), BF16),
            pltpu.VMEM((width, rank), BF16),
            dma((3,)),
            dma((n,)), dma((n,)),
            dma((n, nx)), dma((n, nx)),
            dma((n, nx)), dma((n, nx)),
            dma((nj,)), dma((nj,)),
            dma((nj,)), dma((nj,)),
        ],
        compiler_params=pltpu.CompilerParams(
            collective_id=0, has_side_effects=True, vmem_limit_bytes=67043328 - doubles.size * 2 - 2**16),
        cost_estimate=pl.CostEstimate(
            flops=flops, bytes_accessed=4 * doubles.size, transcendentals=0),
    )(doubles, aux_factors, cycle_factors)


def solution(mesh):
    in_specs = (P(("grp", "ia"), "ja", None, None), P("ia", None, None), P())
    out_specs = P(("grp", "ia"), "ja", None, None)
    body = functools.partial(shards, mesh.shape["ia"], mesh.shape["ja"], mesh.shape["grp"])
    return jax.shard_map(body, mesh=mesh, in_specs=in_specs, out_specs=out_specs, check_vma=False)
```

time: 26.9 us -> 23 us (0.86)
  Pallas kernels: 24.4 us -> 21.8 us
  local copies, waits for them, and re-layouts: 2.4 us -> 1.02 us
    pallas_call x1, Pallas kernels: 24.4 us -> 21.8 us  [shards(): pl.pallas_call(functools.partial(sigma_kernel, n, nj, ny), out_shape=pltp...]
    unnamed x1, local copies, waits for them, and re-layouts: 2.4 us -> 1.02 us
where the time goes in v2:
time: 23 us; the launch traced here: 22.9 us
  Pallas kernels  21.8 us (95%)
  local copies, waits for them, and re-layouts  1.02 us (4%)
    pallas_call x1, Pallas kernels, shards(): pl.pallas_call(functools.partial(sigma_kernel, n, nj, ny), out_shape=pltp...  21.8 us
    unnamed x1, local copies, waits for them, and re-layouts  1.02 us

profile of v2, /device:TPU:0, one launch (start us, length us, event | category | flops | bytes accessed | tf_op | source)
XLA Modules:
  0.0 22.9 jit_solution(14534339885267477921)
XLA Ops:
  0.0 21.8 %shard_map.37 = bf16[1,4,384,384]{3,2,1,0:T(8,128)(2,1)S(1)} custom-call(bf16[1,4,384,384]{3,2,1,0:T(8,128)(2,1)} %d_hbm.1, bf16[1,384,384]{2,1,0:T(8,128)(2,1)} %aux_hbm.1, bf16[16,384,128]{2,1,0:T(8,128)(2,1)} %u_hbm.1), custom_call_target="tpu_custom_call" | custom-call | flops 3925868544 | bytes 2359296 | tf_op jit(solution)/shard_map/pallas_call | solution.py:210
  21.8 1.0 %copy.5 = bf16[1,4,384,384]{3,2,1,0:T(8,128)(2,1)} copy(bf16[1,4,384,384]{3,2,1,0:T(8,128)(2,1)S(1)} %shard_map.37) | data formatting | bytes 2359296
